TPU v7x, 32 devices: a whole 2x2x4 slice. The times are simulated.
32 devices in a mesh: virt: 8 (over z, x), aux: 4 (over y, core).
Axes of the slice: x: 2, y: 2, z: 4, core: 2. Of those that a mesh axis runs over, the one named last changes fastest.
Arguments:
- three_index: bfloat16 [600, 5120], P('aux', 'virt'), may hold values from -0.0625 to 0.0625
- eps_occ: float32 [20], replicated, may hold values from -1.5 to -0.5
- eps_virt: float32 [256], replicated, may hold values from 0.3 to 3
Outputs:
- virt_energy: float32 [256], P('virt')
- pair_energy: float32 [20, 20], replicated
All inputs are finite; a program needn't handle non-finite values.
Results may differ from a plain program's by a relative error of at most 0.0003.
Values may be sent and summed in bfloat16 or wider, within the bound.
A program may use at most 128 MiB of HBM per device.

v0:
```python
import jax
import jax.numpy as jnp
from jax import lax
from jax.sharding import PartitionSpec as P


def on_device(three_index, eps_occ, eps_virt):
    occupied = eps_occ.shape[0]
    own_width = three_index.shape[1] // occupied
    virt_count = lax.axis_size("virt")
    aux_place = lax.axis_index("aux")
    virt_place = lax.axis_index("virt")
    narrow = lax.all_to_all(three_index, "aux", split_axis=1, concat_axis=0, tiled=True)
    partner = lax.all_gather(narrow, "virt", axis=1, tiled=True)
    stride = narrow.shape[1] // occupied
    table = eps_virt.reshape(virt_count, own_width)
    eps_other = lax.dynamic_slice_in_dim(table, aux_place * stride, stride, 1).reshape(-1)
    other_width = partner.shape[1] // occupied
    partner_cube = partner.reshape(partner.shape[0], other_width, occupied)
    eps_own = lax.dynamic_slice_in_dim(eps_virt, virt_place * own_width, own_width)
    incoming = lax.all_gather(three_index, "aux", axis=0, tiled=True)
    rows = incoming.shape[0]
    left_cube = incoming.reshape(rows, own_width, occupied)
    integrals = jnp.einsum(
        "pai,pbj->iajb", left_cube, partner_cube, preferred_element_type=jnp.float32
    )
    denominator = (
        eps_occ[:, None, None, None]
        + eps_occ[None, None, :, None]
        - eps_own[None, :, None, None]
        - eps_other[None, None, None, :]
    )
    swapped = jnp.transpose(integrals, (2, 1, 0, 3))
    energy_terms = integrals * (2.0 * integrals - swapped) / denominator
    virt_local = jnp.sum(energy_terms, axis=(0, 2, 3))
    pair_local = jnp.sum(energy_terms, axis=(1, 3))
    virt_energy, pair_column = lax.psum((virt_local, pair_local), "aux")
    pair_energy = lax.psum(pair_column, "virt")
    return (virt_energy, pair_energy)


def solution(mesh):
    in_specs = (P("aux", "virt"), P(), P())
    out_specs = (P("virt"), P())
    return jax.shard_map(
        on_device, mesh=mesh, in_specs=in_specs, out_specs=out_specs, check_vma=False
    )
```

profile of v0, /device:TPU:0, one launch (start us, length us, event | category | flops | bytes accessed | tf_op | source)
XLA Modules:
  0.0 129.4 jit_solution(3256470533484505875)
XLA Ops:
  7.2 0.0 copy-start
  7.2 0.0 all-gather.3.cloned.1.call-start
  7.2 1.2 all_to_all.14
  8.4 10.6 %all_to_all.19 = bf16[150,4,160]{2,0,1:T(8,128)(2,1)S(1)} all-to-all(bf16[150,4,160]{2,0,1:T(8,128)(2,1)S(1)} %copy.16), channel_id=1, replica_groups=mesh['virt'=8,'aux'=4] {'aux'}, dimensions={1} | all-to-all | bytes 384000 | tf_op jit(solution)/shard_map/all_to_all | solution.py:13
  19.0 0.1 reshape.63
  19.1 0.8 copy.23
  20.0 0.0 all-gather.3.cloned.1.call-update
  20.0 0.8 reshape.57
  20.8 0.8 dynamic_slice.6
  21.5 0.1 constant_dynamic-slice_fusion
  21.6 0.1 sub.41
  21.7 8.4 %all-gather = bf16[4,150,640]{2,1,0:T(8,128)(2,1)S(1)} all-gather(bf16[1,150,640]{2,1,0:T(8,128)(2,1)} %bitcast.31), channel_id=1, replica_groups=mesh['virt'=8,'aux'=4] {'aux'}, dimensions={0}, use_global_device_ids=true | all-gather | bytes 960000 | tf_op jit(solution)/shard_map/all_gather | solution.py:21
  30.0 1.2 copy.18
  31.3 1.1 reshape.56
  32.4 0.0 copy-done
  32.4 0.1 broadcast_add_fusion
  32.5 0.1 broadcast_subtract_fusion
  32.6 32.6 %all-gather.3.cloned.1.call-done = bf16[600,1280]{0,1:T(8,128)(2,1)} async-done(((bf16[600,160]{0,1:T(8,128)(2,1)}), bf16[600,1280]{0,1:T(8,128)(2,1)}) %all-gather.3.cloned.1.call-update) | async-done | bytes 1536016 | tf_op jit(solution)/shard_map/all_gather | solution.py:14
  65.3 2.7 %reshape.55 = bf16[600,64,20]{0,2,1:T(8,128)(2,1)S(1)} reshape(bf16[600,1280]{0,1:T(8,128)(2,1)} %all-gather.3.cloned.1.call-done) | data formatting | bytes 3072000 | tf_op jit(solution)/shard_map/reshape | solution.py:19
  67.9 2.7 %fusion.2 = f32[64,20,32,20]{0,2,3,1:T(8,128)S(1)} fusion(bf16[600,64,20,1]{0,2,1,3:T(8,128)(2,1)S(1)} %bitcast.29, bf16[600,32,20]{0,2,1:T(8,128)(2,1)S(1)} %reshape.56), kind=kOutput, calls=%fused_computation.4 | convolution fusion | flops 983040000 | bytes 5580800 | tf_op jit(solution)/shard_map/pai,pbj->iajb/dot_general | solution.py:24
  70.7 6.5 %fusion.6 = (f32[20,20]{1,0:T(8,128)S(1)}, f32[32]{0:T(128)S(1)}) fusion(f32[64]{0:T(128)S(1)} %sub.41, f32[20,32,20]{1,2,0:T(8,128)S(1)} %broadcast_subtract_fusion, f32[64,20,32,20]{0,2,3,1:T(8,128)S(1)} %fusion.2), kind=kLoop, calls=%fused_computation.8 | loop fusion | flops 5733968 | bytes 3329984 | tf_op jit(solution)/shard_map/reduce_sum | solution.py:36
  77.2 10.6 %all-reduce = (f32[32]{0:T(128)}, f32[20,20]{1,0:T(8,128)S(1)}) all-reduce(f32[32]{0:T(128)S(1)} %get-tuple-element.3, f32[20,20]{1,0:T(8,128)S(1)} %get-tuple-element.2), channel_id=1, replica_groups=mesh['virt'=8,'aux'=4] {'aux'}, use_global_device_ids=true, to_apply=%region_1.0 | all-reduce | flops 432 | bytes 3456 | tf_op jit(solution)/shard_map/psum | solution.py:37
  87.8 34.8 %psum.23 = f32[20,20]{1,0:T(8,128)} all-reduce(f32[20,20]{1,0:T(8,128)S(1)} %get-tuple-element.5), channel_id=1, replica_groups=mesh['virt'=8,'aux'=4] {'virt'}, use_global_device_ids=true, to_apply=%region_4.0 | all-reduce | flops 400 | bytes 3200 | tf_op jit(solution)/shard_map/psum | solution.py:38
  (1 shorter events, 0.0 us)
Async XLA Ops:
  7.2 25.2 %copy-start = (f32[20]{0:T(128)S(1)}, f32[20]{0:T(128)}, u32[]{:S(2)}) copy-start(f32[20]{0:T(128)} %param.4) | copy-start | bytes 244
  7.2 58.1 %all-gather.3.cloned.1.call-start = ((), (), s32[]{:S(2)}) async-start(), calls=%async_computation.1 | async-start | bytes 1843200 | tf_op jit(solution)/shard_map/all_gather | solution.py:14
Sparse Core Ops, SparseCore 0:
  20.1 45.0 all-gather.2
where the time goes:
time: 130 us; the launch traced here: 129 us
  blocking collectives  64.4 us (50%)
  waiting for transfers between devices  32.7 us (25%)
  between operations  14.1 us (11%)
  local copies, waits for them, and re-layouts  8.83 us (7%)
  other arithmetic  6.69 us (5%)
  matrix products  2.73 us (2%)
    psum x1, blocking collectives, on_device(): pair_energy = lax.psum(pair_column, 'virt')  34.8 us
    all_gather x1, waiting for transfers between devices, on_device(): partner = lax.all_gather(narrow, 'virt', axis=1, tiled=True)  32.6 us
    psum x1, blocking collectives, on_device(): virt_energy, pair_column = lax.psum((virt_local, pair_local), 'aux')  10.6 us
    all_to_all x1, blocking collectives, on_device(): lax.all_to_all(three_index, 'aux', split_axis=1, concat_axis=0, tiled=True)  10.6 us
    all_gather x1, blocking collectives, on_device(): incoming = lax.all_gather(three_index, 'aux', axis=0, tiled=True)  8.36 us
    reduce_sum x1, other arithmetic, on_device(): pair_local = jnp.sum(energy_terms, axis=(1, 3))  6.49 us
    dot_general x1, matrix products, on_device(): jnp.einsum('pai,pbj->iajb', left_cube, partner_cube, preferred_element_ty...  2.73 us
    reshape x1, local copies, waits for them, and re-layouts, on_device(): partner_cube = partner.reshape(partner.shape[0], other_width, occupied)  2.67 us
  transfers between devices with their start and end apart: 1, of which 1 were waited for; matrix products, arithmetic and copies ran while one was open for 3% of the time, Pallas kernels for 0%

commit v1 on v0

--- a/solution.py
+++ b/solution.py
@@ -35,7 +35,7 @@
     virt_local = jnp.sum(energy_terms, axis=(0, 2, 3))
     pair_local = jnp.sum(energy_terms, axis=(1, 3))
     virt_energy, pair_column = lax.psum((virt_local, pair_local), "aux")
-    pair_energy = lax.psum(pair_column, "virt")
+    pair_energy = jnp.sum(lax.all_gather(pair_column, "virt"), axis=0)
     return (virt_energy, pair_energy)
 
 

time: 130 us -> 126 us (0.969)
  blocking collectives: 64.4 us -> 60.1 us
    psum x1 -> x0, blocking collectives: 34.8 us -> none  [on_device(): pair_energy = lax.psum(pair_column, 'virt')]
    all_gather x0 -> x1, blocking collectives: none -> 30.5 us  [on_device(): pair_energy = jnp.sum(lax.all_gather(pair_column, 'virt'), axis=0)]
where the time goes in v1:
time: 126 us
  blocking collectives  60.1 us (48%)
  waiting for transfers between devices  32.7 us (26%)
  between operations  14.1 us (11%)
  local copies, waits for them, and re-layouts  8.83 us (7%)
  other arithmetic  7.3 us (6%)
  matrix products  2.73 us (2%)
    all_gather x1, waiting for transfers between devices, on_device(): partner = lax.all_gather(narrow, 'virt', axis=1, tiled=True)  32.6 us
    all_gather x1, blocking collectives, on_device(): pair_energy = jnp.sum(lax.all_gather(pair_column, 'virt'), axis=0)  30.5 us
    psum x1, blocking collectives, on_device(): virt_energy, pair_column = lax.psum((virt_local, pair_local), 'aux')  10.6 us
    all_to_all x1, blocking collectives, on_device(): lax.all_to_all(three_index, 'aux', split_axis=1, concat_axis=0, tiled=True)  10.6 us
    all_gather x1, blocking collectives, on_device(): incoming = lax.all_gather(three_index, 'aux', axis=0, tiled=True)  8.36 us
    reduce_sum x1, other arithmetic, on_device(): pair_local = jnp.sum(energy_terms, axis=(1, 3))  6.49 us
    dot_general x1, matrix products, on_device(): jnp.einsum('pai,pbj->iajb', left_cube, partner_cube, preferred_element_ty...  2.73 us
    reshape x1, local copies, waits for them, and re-layouts, on_device(): partner_cube = partner.reshape(partner.shape[0], other_width, occupied)  2.67 us
  transfers between devices with their start and end apart: 1, of which 1 were waited for; matrix products, arithmetic and copies ran while one was open for 3% of the time, Pallas kernels for 0%

profile of v1, /device:TPU:0, one launch (start us, length us, event | category | flops | bytes accessed | tf_op | source)
XLA Modules:
  0.0 125.8 jit_solution(13522278502170953506)
XLA Ops:
  7.2 0.0 copy-start
  7.2 0.0 all-gather.3.cloned.1.call-start
  7.2 1.2 all_to_all.14
  8.4 10.6 %all_to_all.19 = bf16[150,4,160]{2,0,1:T(8,128)(2,1)S(1)} all-to-all(bf16[150,4,160]{2,0,1:T(8,128)(2,1)S(1)} %copy.16), channel_id=1, replica_groups=mesh['virt'=8,'aux'=4] {'aux'}, dimensions={1} | all-to-all | bytes 384000 | tf_op jit(solution)/shard_map/all_to_all | solution.py:13
  19.0 0.1 reshape.63
  19.1 0.8 copy.23
  20.0 0.0 all-gather.3.cloned.1.call-update
  20.0 0.8 reshape.57
  20.8 0.8 dynamic_slice.6
  21.5 0.1 constant_dynamic-slice_fusion
  21.6 0.1 sub.41
  21.7 8.4 %all-gather = bf16[4,150,640]{2,1,0:T(8,128)(2,1)S(1)} all-gather(bf16[1,150,640]{2,1,0:T(8,128)(2,1)} %bitcast.32), channel_id=1, replica_groups=mesh['virt'=8,'aux'=4] {'aux'}, dimensions={0}, use_global_device_ids=true | all-gather | bytes 960000 | tf_op jit(solution)/shard_map/all_gather | solution.py:21
  30.0 1.2 copy.18
  31.3 1.1 reshape.56
  32.4 0.0 copy-done
  32.4 0.1 broadcast_add_fusion
  32.5 0.1 broadcast_subtract_fusion
  32.6 32.6 %all-gather.3.cloned.1.call-done = bf16[600,1280]{0,1:T(8,128)(2,1)} async-done(((bf16[600,160]{0,1:T(8,128)(2,1)}), bf16[600,1280]{0,1:T(8,128)(2,1)}) %all-gather.3.cloned.1.call-update) | async-done | bytes 1536016 | tf_op jit(solution)/shard_map/all_gather | solution.py:14
  65.3 2.7 %reshape.55 = bf16[600,64,20]{0,2,1:T(8,128)(2,1)S(1)} reshape(bf16[600,1280]{0,1:T(8,128)(2,1)} %all-gather.3.cloned.1.call-done) | data formatting | bytes 3072000 | tf_op jit(solution)/shard_map/reshape | solution.py:19
  67.9 2.7 %fusion.2 = f32[64,20,32,20]{0,2,3,1:T(8,128)S(1)} fusion(bf16[600,64,20,1]{0,2,1,3:T(8,128)(2,1)S(1)} %bitcast.30, bf16[600,32,20]{0,2,1:T(8,128)(2,1)S(1)} %reshape.56), kind=kOutput, calls=%fused_computation.4 | convolution fusion | flops 983040000 | bytes 5580800 | tf_op jit(solution)/shard_map/pai,pbj->iajb/dot_general | solution.py:24
  70.7 6.5 %fusion.6 = (f32[20,20]{1,0:T(8,128)S(1)}, f32[32]{0:T(128)S(1)}) fusion(f32[64]{0:T(128)S(1)} %sub.41, f32[20,32,20]{1,2,0:T(8,128)S(1)} %broadcast_subtract_fusion, f32[64,20,32,20]{0,2,3,1:T(8,128)S(1)} %fusion.2), kind=kLoop, calls=%fused_computation.8 | loop fusion | flops 5733968 | bytes 3329984 | tf_op jit(solution)/shard_map/reduce_sum | solution.py:36
  77.2 10.6 %all-reduce = (f32[32]{0:T(128)}, f32[1,20,20]{2,1,0:T(8,128)S(1)}) all-reduce(f32[32]{0:T(128)S(1)} %get-tuple-element.3, f32[1,20,20]{2,1,0:T(8,128)S(1)} %bitcast.33), channel_id=1, replica_groups=mesh['virt'=8,'aux'=4] {'aux'}, use_global_device_ids=true, to_apply=%region_1.0 | all-reduce | flops 432 | bytes 3456 | tf_op jit(solution)/shard_map/psum | solution.py:37
  87.8 30.5 %all_gather.15 = f32[8,20,20]{2,1,0:T(8,128)S(1)} all-gather(f32[1,20,20]{2,1,0:T(8,128)S(1)} %get-tuple-element.5), channel_id=1, replica_groups=mesh['virt'=8,'aux'=4] {'virt'}, dimensions={0}, use_global_device_ids=true | all-gather | bytes 14400 | tf_op jit(solution)/shard_map/all_gather | solution.py:38
  118.4 0.6 reduce_sum.29
  (1 shorter events, 0.0 us)
Async XLA Ops:
  7.2 25.2 %copy-start = (f32[20]{0:T(128)S(1)}, f32[20]{0:T(128)}, u32[]{:S(2)}) copy-start(f32[20]{0:T(128)} %param.4) | copy-start | bytes 244
  7.2 58.1 %all-gather.3.cloned.1.call-start = ((), (), s32[]{:S(2)}) async-start(), calls=%async_computation.1 | async-start | bytes 1843200 | tf_op jit(solution)/shard_map/all_gather | solution.py:14
Sparse Core Ops, SparseCore 0:
  20.1 45.0 all-gather.2
